TPU v7x, 16 devices: a whole 2x2x2 slice. The times are simulated.
16 devices in a mesh: fsdp: 16 (over z, y, x, core).
Axes of the slice: x: 2, y: 2, z: 2, core: 2. Of those that a mesh axis runs over, the one named last changes fastest.
Arguments:
- token_ids: int32 [64, 512], P('fsdp')
- grad_y: bfloat16 [64, 512, 896], P('fsdp')
- table: bfloat16 [151936, 896], P('fsdp')
- norm1_gain: bfloat16 [896], P('fsdp')
- norm2_gain: bfloat16 [896], P('fsdp')
- w_query: bfloat16 [896, 14, 64], P('fsdp')
- w_key: bfloat16 [896, 2, 64], P('fsdp')
- w_value: bfloat16 [896, 2, 64], P('fsdp')
- w_out: bfloat16 [896, 896], P('fsdp')
- w_gate: bfloat16 [896, 4864], P('fsdp')
- w_up: bfloat16 [896, 4864], P('fsdp')
- w_down: bfloat16 [4864, 896], P('fsdp')
Outputs:
- output 1: bfloat16 [64, 512, 896], P('fsdp')
- output 2: bfloat16 [151936, 896], P('fsdp')
- output 3: bfloat16 [896], P('fsdp')
- output 4: bfloat16 [896], P('fsdp')
- output 5: bfloat16 [896, 14, 64], P('fsdp')
- output 6: bfloat16 [896, 2, 64], P('fsdp')
- output 7: bfloat16 [896, 2, 64], P('fsdp')
- output 8: bfloat16 [896, 896], P('fsdp')
- output 9: bfloat16 [896, 4864], P('fsdp')
- output 10: bfloat16 [896, 4864], P('fsdp')
- output 11: bfloat16 [4864, 896], P('fsdp')
All inputs are finite; a program needn't handle non-finite values.
Results may differ from a plain program's by a relative error of at most 0.0156515.
Values are sent between devices in bfloat16 or wider.
A program may use at most 1 GiB of HBM per device.

v0:
```python
import jax
import jax.numpy as jnp
from jax import lax
from jax.sharding import PartitionSpec as P

AXIS_NAME = "fsdp"
NORM_EPS = 1e-5
ROPE_THETA = 500000.0


def rms_norm(x_f32, gain_f32):
    inv_rms = lax.rsqrt(jnp.mean(x_f32 * x_f32, axis=-1, keepdims=True) + NORM_EPS)
    return (x_f32 * inv_rms * gain_f32).astype(jnp.bfloat16)


def rotary(x_f32):
    head_dim = x_f32.shape[-1]
    half_dim = head_dim // 2
    seq_len = x_f32.shape[-3]
    inv_freq = ROPE_THETA ** (-2.0 * jnp.arange(half_dim, dtype=jnp.float32) / head_dim)
    angles = jnp.arange(seq_len, dtype=jnp.float32)[:, None] * inv_freq[None, :]
    cos_tab = jnp.cos(angles)[:, None, :]
    sin_tab = jnp.sin(angles)[:, None, :]
    lo_half = x_f32[..., :half_dim]
    hi_half = x_f32[..., half_dim:]
    return jnp.concatenate([lo_half * cos_tab - hi_half * sin_tab, hi_half * cos_tab + lo_half * sin_tab], axis=-1)


def attend(q_f32, k_f32, v_bf16):
    batch_loc, seq_len, q_heads, head_dim = q_f32.shape
    kv_heads = k_f32.shape[2]
    q_rot = rotary(q_f32).astype(jnp.bfloat16).reshape(batch_loc, seq_len, kv_heads, q_heads // kv_heads, head_dim)
    k_rot = rotary(k_f32).astype(jnp.bfloat16)
    scores = jnp.einsum("bqkgd,bskd->bkgqs", q_rot, k_rot, preferred_element_type=jnp.float32) * head_dim ** -0.5
    positions = jnp.arange(seq_len)
    causal = positions[:, None] >= positions[None, :]
    scores = jnp.where(causal, scores, -1e30)
    prob_bf = jax.nn.softmax(scores, axis=-1).astype(jnp.bfloat16)
    attn_out = jnp.einsum("bkgqs,bskd->bqkgd", prob_bf, v_bf16, preferred_element_type=jnp.float32)
    return attn_out.astype(jnp.bfloat16).reshape(batch_loc, seq_len, q_heads * head_dim)


def gated(gate_f32, up_f32):
    return (jax.nn.silu(gate_f32) * up_f32).astype(jnp.bfloat16)


def layer_pass(emb_rows, grad_y, norm1_gain, norm2_gain, w_query, w_key, w_value, w_out, w_gate, w_up, w_down):
    x_f32 = emb_rows.astype(jnp.float32)
    h_one, norm1_pull = jax.vjp(rms_norm, x_f32, norm1_gain.astype(jnp.float32))
    q_f32 = jnp.einsum("bsd,dhe->bshe", h_one, w_query, preferred_element_type=jnp.float32)
    k_f32 = jnp.einsum("bsd,dhe->bshe", h_one, w_key, preferred_element_type=jnp.float32)
    v_bf16 = jnp.einsum("bsd,dhe->bshe", h_one, w_value, preferred_element_type=jnp.float32).astype(jnp.bfloat16)
    attn_out, attn_pull = jax.vjp(attend, q_f32, k_f32, v_bf16)
    resid_f32 = x_f32 + jnp.einsum("bse,ed->bsd", attn_out, w_out, preferred_element_type=jnp.float32)
    resid_two = resid_f32.astype(jnp.bfloat16).astype(jnp.float32)
    h_two, norm2_pull = jax.vjp(rms_norm, resid_two, norm2_gain.astype(jnp.float32))
    gate_f32 = jnp.einsum("bsd,df->bsf", h_two, w_gate, preferred_element_type=jnp.float32)
    up_f32 = jnp.einsum("bsd,df->bsf", h_two, w_up, preferred_element_type=jnp.float32)
    act_bf16, act_pull = jax.vjp(gated, gate_f32, up_f32)
    layer_out = (resid_two + jnp.einsum("bsf,fd->bsd", act_bf16, w_down, preferred_element_type=jnp.float32)).astype(jnp.bfloat16)
    g_down = jnp.einsum("bsf,bsd->fd", act_bf16, grad_y, preferred_element_type=jnp.float32)
    d_act = jnp.einsum("bsd,fd->bsf", grad_y, w_down, preferred_element_type=jnp.float32).astype(jnp.bfloat16)
    d_gate, d_up = act_pull(d_act)
    d_gate = d_gate.astype(jnp.bfloat16)
    d_up = d_up.astype(jnp.bfloat16)
    g_gate = jnp.einsum("bsd,bsf->df", h_two, d_gate, preferred_element_type=jnp.float32)
    g_up = jnp.einsum("bsd,bsf->df", h_two, d_up, preferred_element_type=jnp.float32)
    d_h_two = (jnp.einsum("bsf,df->bsd", d_gate, w_gate, preferred_element_type=jnp.float32) + jnp.einsum("bsf,df->bsd", d_up, w_up, preferred_element_type=jnp.float32)).astype(jnp.bfloat16)
    d_resid_two, g_norm2 = norm2_pull(d_h_two)
    d_resid = (grad_y.astype(jnp.float32) + d_resid_two).astype(jnp.bfloat16)
    g_out = jnp.einsum("bse,bsd->ed", attn_out, d_resid, preferred_element_type=jnp.float32)
    d_attn = jnp.einsum("bsd,ed->bse", d_resid, w_out, preferred_element_type=jnp.float32).astype(jnp.bfloat16)
    d_query, d_key, d_value = attn_pull(d_attn)
    d_query = d_query.astype(jnp.bfloat16)
    d_key = d_key.astype(jnp.bfloat16)
    g_query = jnp.einsum("bsd,bshe->dhe", h_one, d_query, preferred_element_type=jnp.float32)
    g_key = jnp.einsum("bsd,bshe->dhe", h_one, d_key, preferred_element_type=jnp.float32)
    g_value = jnp.einsum("bsd,bshe->dhe", h_one, d_value, preferred_element_type=jnp.float32)
    d_h_one = (jnp.einsum("bshe,dhe->bsd", d_query, w_query, preferred_element_type=jnp.float32) + jnp.einsum("bshe,dhe->bsd", d_key, w_key, preferred_element_type=jnp.float32) + jnp.einsum("bshe,dhe->bsd", d_value, w_value, preferred_element_type=jnp.float32)).astype(jnp.bfloat16)
    d_x, g_norm1 = norm1_pull(d_h_one)
    d_emb = (d_resid.astype(jnp.float32) + d_x).astype(jnp.bfloat16)
    return layer_out, d_emb, (g_norm1, g_norm2, g_query, g_key, g_value, g_out, g_gate, g_up, g_down)


def solution(mesh):
    spec_1d = P(AXIS_NAME)
    spec_2d = P(AXIS_NAME, None)
    spec_3d = P(AXIS_NAME, None, None)
    in_specs = (spec_2d, spec_3d, spec_2d, spec_1d, spec_1d, spec_3d, spec_3d, spec_3d, spec_2d, spec_2d, spec_2d, spec_2d)
    out_specs = (spec_3d, spec_2d, spec_1d, spec_1d, spec_3d, spec_3d, spec_3d, spec_2d, spec_2d, spec_2d, spec_2d)

    def device_step(token_ids, grad_y, table, *weight_shards):
        ids_all = lax.all_gather(token_ids, AXIS_NAME, axis=0, tiled=True)
        rows_dev = table.shape[0]
        rel_ids = ids_all - lax.axis_index(AXIS_NAME) * rows_dev
        owned = (rel_ids >= 0) & (rel_ids < rows_dev)
        picked = jnp.take(table, jnp.where(owned, rel_ids, 0), axis=0)
        part_emb = jnp.where(owned[:, :, None], picked, jnp.zeros((), jnp.bfloat16))
        emb_rows = lax.psum_scatter(part_emb, AXIS_NAME, scatter_dimension=0, tiled=True)
        full_weights = [lax.all_gather(w_shard, AXIS_NAME, axis=0, tiled=True) for w_shard in weight_shards]
        layer_out, d_emb, partials = layer_pass(emb_rows, grad_y, *full_weights)
        grads = [lax.psum_scatter(part_grad, AXIS_NAME, scatter_dimension=0, tiled=True).astype(jnp.bfloat16) for part_grad in partials]
        d_emb_all = lax.all_gather(d_emb, AXIS_NAME, axis=0, tiled=True)
        seg_ids = jnp.where(owned, rel_ids, rows_dev).reshape(-1)
        d_rows = jax.ops.segment_sum(d_emb_all.reshape(-1, d_emb_all.shape[-1]).astype(jnp.float32), seg_ids, num_segments=rows_dev)
        return tuple([layer_out, d_rows.astype(jnp.bfloat16)] + grads)

    return jax.shard_map(device_step, mesh=mesh, in_specs=in_specs, out_specs=out_specs, check_vma=False)
```

profile of v0, /device:TPU:0, one launch (start us, length us, event | category | flops | bytes accessed | tf_op | source)
XLA Modules:
  0.0 2502.3 jit_solution(9140476954056606649)
XLA Ops:
  8.0 15.1 all-gather
  23.9 158.9 %gather_fusion = bf16[32768,896]{1,0:T(8,128)(2,1)} fusion(bf16[9496,896]{1,0:T(8,128)(2,1)} %param.14, s32[32768]{0:T(1024)S(1)} %broadcast_clamp_fusion), kind=kCustom, calls=%fused_computation | custom fusion | bytes 117571584 | tf_op jit(solution)/shard_map/jit(_take)/gather | solution.py:97
  182.9 39.3 %select_select_fusion = bf16[64,512,896]{2,1,0:T(8,128)(2,1)} fusion(bf16[64,512,896]{2,1,0:T(8,128)(2,1)} %bitcast.206, pred[64,512]{1,0:T(8,128)(4,1)S(1)} %get-tuple-element.66, pred[64,512]{1,0:T(8,128)(4,1)S(1)} %get-tuple-element.65), kind=kLoop, calls=%fused_computation.17 | loop fusion | flops 58720256 | bytes 117506048 | tf_op jit(solution)/shard_map/jit(_where)/select_n | solution.py:98
  226.1 32.6 %all-reduce.10 = (bf16[896]{0:T(1024)(128)(2,1)S(1)}, bf16[896]{0:T(1024)(128)(2,1)S(1)}) all-reduce(bf16[896]{0:T(1024)(128)(2,1)S(1)} %dynamic-update-slice, bf16[896]{0:T(1024)(128)(2,1)S(1)} %dynamic-update-slice.1), channel_id=1, replica_groups=mesh['fsdp'=16] {'fsdp'}, use_global_device_ids=true, to_apply=%add.4 | all-reduce | flops 1792 | bytes 7168
  258.8 14.5 all_gather.36
  273.7 13.7 all_gather.35
  287.4 27.7 %convolution_convert_fusion.1 = bf16[4,512,4864]{2,1,0:T(8,128)(2,1)} fusion(bf16[4,512,896]{2,1,0:T(8,128)(2,1)} %param.13, bf16[4864,896]{1,0:T(8,128)(2,1)} %all-gather.16.cloned.1.call-done), kind=kOutput, calls=%fused_computation.41 | convolution fusion | flops 17860919296 | bytes 32309248 | tf_op jit(solution)/shard_map/bsd,fd->bsf/dot_general | solution.py:62
  315.1 510.7 %reduce-scatter.12.cloned.1.call-done = bf16[4,512,896]{2,1,0:T(8,128)(2,1)} async-done(((bf16[64,512,896]{2,1,0:T(8,128)(2,1)}), bf16[4,512,896]{2,1,0:T(8,128)(2,1)}) %reduce-scatter.12.cloned.1.call-update) | async-done | bytes 3670032 | tf_op jit(solution)/shard_map/reduce_scatter | solution.py:99
  825.8 2.8 fusion.40
  828.6 3.5 fusion.73
  832.4 26.3 %all-gather.8.cloned.1.call-done = bf16[896,14,64]{2,0,1:T(8,128)(2,1)} async-done(((bf16[56,14,64]{2,0,1:T(8,128)(2,1)}), bf16[896,14,64]{2,0,1:T(8,128)(2,1)}) %all-gather.8.cloned.1.call-update) | async-done | bytes 1605648 | tf_op jit(solution)/shard_map/all_gather | solution.py:100
  858.7 7.3 fusion.52
  867.3 20.8 fusion.9
  889.7 19.4 fusion.15
  909.1 29.7 %divide_convert_fusion = bf16[4,2,7,512,512]{3,4,2,1,0:T(8,128)(2,1)} fusion(f32[4,2,512,512,7]{3,2,4,1,0:T(8,128)} %get-tuple-element.70, f32[4,2,7,512]{3,2,1,0:T(8,128)S(1)} %fusion.15, f32[4,2,7,512]{3,2,1,0:T(8,128)S(1)} %get-tuple-element.69, pred[512,512]{0,1:T(8,128)(4,1)S(1)} %iota_compare_fusion.1), kind=kLoop, calls=%fused_computation.15 | loop fusion | flops 73400320 | bytes 88571904 | tf_op jit(solution)/shard_map/jvp()/convert_element_type | solution.py:38
  938.8 16.3 convolution_convert_fusion.3
  955.1 10.3 fusion.43
  966.1 29.5 %fusion.26 = f32[4,512,4864]{2,1,0:T(8,128)} fusion(bf16[896,4864]{1,0:T(8,128)(2,1)} %all-gather.14.cloned.1.call-done, bf16[4,512,896]{2,1,0:T(8,128)(2,1)} %get-tuple-element.72, f32[896]{0:T(1024)S(1)} %convert_element_type.176, f32[4,512]{1,0:T(4,128)S(1)} %fusion.81), kind=kOutput, calls=%fused_computation.60 | convolution fusion | flops 17858297856 | bytes 52243968 | tf_op jit(solution)/shard_map/bsd,df->bsf/dot_general | solution.py:58
  995.7 51.9 %fusion.13 = (bf16[4,512,4864]{2,1,0:T(8,128)(2,1)}, bf16[4,512,4864]{2,1,0:T(8,128)(2,1)}, bf16[4,512,4864]{2,1,0:T(8,128)(2,1)}) fusion(f32[4,512,4864]{2,1,0:T(8,128)} %fusion.26, bf16[4,512,4864]{2,1,0:T(8,128)(2,1)} %convolution_convert_fusion.1, bf16[896,4864]{1,0:T(8,128)(2,1)} %all-gather.12.cloned.1.call-done, ...), kind=kOutput, calls=%fused_computation.24 | convolution fusion | flops 18027642880 | bytes 131935744 | tf_op jit(solution)/shard_map/bsd,df->bsf/dot_general | solution.py:57
  1047.6 27.9 %fusion.24 = f32[4,512,896]{2,1,0:T(8,128)} fusion(bf16[4,512,4864]{2,1,0:T(8,128)(2,1)} %get-tuple-element.54, bf16[896,4864]{1,0:T(8,128)(2,1)} %all-gather.14.cloned.1.call-done), kind=kOutput, calls=%fused_computation.58 | convolution fusion | flops 17850957824 | bytes 35979264 | tf_op jit(solution)/shard_map/bsf,df->bsd/dot_general | solution.py:68
  1075.4 29.9 %fusion.34 = (f32[896]{0:T(1024)}, f32[4,512]{1,0:T(4,128)S(1)}, bf16[4,512,896]{2,1,0:T(8,128)(2,1)}) fusion(bf16[4,512,896]{2,1,0:T(8,128)(2,1)S(1)} %copy-done.16, f32[4,512]{1,0:T(4,128)S(1)} %fusion.81, f32[896]{0:T(1024)S(1)} %convert_element_type.176, f32[4,512,896]{2,1,0:T(8,128)} %fusion.24, bf16[4,512,4864]{2,1,0:T(8,128)(2,1)} %get-tuple-element.52, ...), kind=kOutput, calls=%fused_computation.68 | convolution fusion | flops 17869305856 | bytes 43342848 | tf_op jit(solution)/shard_map/bsf,df->bsd/dot_general | solution.py:68
  1105.4 4.1 fusion.37
  1111.3 5.8 convolution_convert_fusion.2
  1117.1 6.0 copy.61
  1123.1 14.5 fusion.66
  1138.5 2.6 convolution_bitcast_fusion.6
  1141.3 36.6 %fusion.8 = (f32[4,2,7,512]{3,2,1,0:T(8,128)S(1)}, bf16[4,2,7,512,512]{3,4,2,1,0:T(8,128)(2,1)}) fusion(f32[4,2,512,512,7]{3,2,4,1,0:T(8,128)} %get-tuple-element.70, f32[4,2,7,512]{3,2,1,0:T(8,128)S(1)} %copy-done.49, f32[4,2,7,512]{3,2,1,0:T(8,128)S(1)} %copy-done.36, pred[512,512]{0,1:T(8,128)(4,1)S(1)} %copy-done.18, ...), kind=kOutput, calls=%fused_computation.13 | convolution fusion | flops 1996460032 | bytes 92880896 | tf_op jit(solution)/shard_map/transpose(jvp(bkgqs,bskd->bqkgd))/dot_general | solution.py:39
  1177.9 39.2 %fusion.6 = bf16[4,2,512,512,7]{3,2,4,1,0:T(8,128)(2,1)} fusion(bf16[4,2,7,512,512]{3,4,2,1,0:T(8,128)(2,1)} %get-tuple-element.75, f32[4,2,512,512,7]{3,2,4,1,0:T(8,128)} %get-tuple-element.70, f32[4,2,512,7]{2,3,1,0:T(8,128)S(1)} %bitcast.218, f32[4,2,512,7]{2,3,1,0:T(8,128)S(1)} %negate_bitcast_fusion, f32[4,2,512,7]{2,3,1,0:T(8,128)S(1)} %bitcast.217, ...), kind=kLoop, calls=%fused_computation.11 | loop fusion | flops 146800640 | bytes 118046720 | tf_op jit(solution)/shard_map/transpose(jvp())/mul | solution.py:34
  1217.1 13.5 fusion.64
  1231.9 2.6 convolution_bitcast_fusion.7
  1234.6 8.8 convolution_bitcast_fusion.4
  1243.5 11.7 convert_convert_fusion
  1260.1 10.5 convolution_bitcast_fusion.3
  1270.7 26.2 %convolution_bitcast_fusion.1 = f32[896,4864]{1,0:T(8,128)} fusion(bf16[4,512,4864]{2,1,0:T(8,128)(2,1)} %get-tuple-element.54, bf16[4,512,896]{2,1,0:T(8,128)(2,1)} %get-tuple-element.72, f32[896]{0:T(1024)S(1)} %copy-done.59, f32[4,512]{1,0:T(4,128)S(1)} %copy-done.53), kind=kOutput, calls=%fused_computation.45 | convolution fusion | flops 17858297856 | bytes 41037312 | tf_op jit(solution)/shard_map/bsd,bsf->df/dot_general | solution.py:67
  1296.9 26.3 %convolution_bitcast_fusion.2 = f32[896,4864]{1,0:T(8,128)} fusion(bf16[4,512,4864]{2,1,0:T(8,128)(2,1)} %get-tuple-element.52, bf16[4,512,896]{2,1,0:T(8,128)(2,1)} %get-tuple-element.72, f32[896]{0:T(1024)S(1)} %copy-done.59, f32[4,512]{1,0:T(4,128)S(1)} %copy-done.53), kind=kOutput, calls=%fused_computation.46 | convolution fusion | flops 17858297856 | bytes 41037312 | tf_op jit(solution)/shard_map/bsd,bsf->df/dot_general | solution.py:66
  1323.3 28.3 %convolution_bitcast_fusion = f32[4864,896]{1,0:T(8,128)} fusion(bf16[4,512,4864]{2,1,0:T(8,128)(2,1)} %get-tuple-element.53, bf16[4,512,896]{2,1,0:T(8,128)(2,1)} %param.13), kind=kOutput, calls=%fused_computation.44 | convolution fusion | flops 17850957824 | bytes 41025536 | tf_op jit(solution)/shard_map/bsf,bsd->fd/dot_general | solution.py:61
  1356.1 11.6 fusion.50
  1367.8 6.3 fusion.35
  1374.2 3.7 fusion.39
  1378.0 32.9 %all-reduce.9 = (bf16[896]{0:T(1024)(128)(2,1)S(1)}, bf16[896]{0:T(1024)(128)(2,1)S(1)}) all-reduce(f32[896]{0:T(1024)S(1)} %get-tuple-element.46, f32[896]{0:T(1024)S(1)} %copy-done.60), channel_id=3, replica_groups=mesh['fsdp'=16] {'fsdp'}, use_global_device_ids=true, to_apply=%region_10.11.clone | all-reduce | flops 1792 | bytes 10752
  1412.0 27.6 %fusion.44 = bf16[4,512,896]{2,1,0:T(8,128)(2,1)} fusion(bf16[4,512,896]{2,1,0:T(8,128)(2,1)} %get-tuple-element.72, bf16[4,512,4864]{2,1,0:T(8,128)(2,1)} %get-tuple-element.53, bf16[4864,896]{1,0:T(8,128)(2,1)} %all-gather.16.cloned.1.call-done), kind=kOutput, calls=%fused_computation.78 | convolution fusion | flops 17856462848 | bytes 35979264 | tf_op jit(solution)/shard_map/bsf,fd->bsd/dot_general | solution.py:60
  1445.8 166.2 %reduce-scatter.22.cloned.1.call-done = f32[56,4864]{1,0:T(8,128)} async-done(((f32[896,4864]{1,0:T(8,128)}), f32[56,4864]{1,0:T(8,128)}) %reduce-scatter.22.cloned.1.call-update) | async-done | bytes 1089552 | tf_op jit(solution)/shard_map/reduce_scatter | solution.py:102
  1612.0 2.1 convert_element_type.218
  1614.1 182.2 %reduce-scatter.20.cloned.1.call-done = f32[56,4864]{1,0:T(8,128)} async-done(((f32[896,4864]{1,0:T(8,128)}), f32[56,4864]{1,0:T(8,128)}) %reduce-scatter.20.cloned.1.call-update) | async-done | bytes 1089552 | tf_op jit(solution)/shard_map/reduce_scatter | solution.py:102
  1798.4 182.3 %reduce-scatter.24.cloned.1.call-done = f32[304,896]{1,0:T(8,128)} async-done(((f32[4864,896]{1,0:T(8,128)}), f32[304,896]{1,0:T(8,128)}) %reduce-scatter.24.cloned.1.call-update) | async-done | bytes 1089552 | tf_op jit(solution)/shard_map/reduce_scatter | solution.py:102
  1982.8 212.4 %all-gather.18.cloned.1.call-done = bf16[64,512,896]{2,1,0:T(8,128)(2,1)} async-done(((bf16[4,512,896]{2,1,0:T(8,128)(2,1)}), bf16[64,512,896]{2,1,0:T(8,128)(2,1)}) %all-gather.18.cloned.1.call-update) | async-done | bytes 58720272 | tf_op jit(solution)/shard_map/all_gather | solution.py:103
  2195.2 282.7 %scatter_custom_fusion = f32[9496,896]{1,0:T(8,128)} fusion(s32[32768]{0:T(1024)S(1)} %bitcast.222, bf16[32768,896]{1,0:T(8,128)(2,1)} %bitcast.207, f32[]{:T(128)} %constant.22.clone.1), kind=kCustom, calls=%fused_computation.2 | custom fusion | flops 58720256 | bytes 92753920 | tf_op jit(solution)/shard_map/scatter-add | solution.py:105
  2477.9 17.4 convert_element_type.210
  (205 shorter events, 34.6 us)
Async XLA Ops:
  7.2 280.2 %all-gather.16.cloned.1.call-start = ((), (), s32[]{:S(2)}) async-start(), calls=%async_computation.13 | async-start | bytes 9261056 | tf_op jit(solution)/shard_map/all_gather | solution.py:100
  7.9 817.9 %reduce-scatter.12.cloned.1.call-start = ((), (), s32[]{:S(2)}) async-start(), calls=%async_computation.8 | async-start | bytes 62390272 | tf_op jit(solution)/shard_map/reduce_scatter | solution.py:99
  222.2 36.6 %copy-start.56 = (bf16[56,2,64]{2,1,0:T(2,128)(2,1)S(1)}, bf16[56,2,64]{2,1,0:T(2,128)(2,1)}, u32[]{:S(2)}) copy-start(bf16[56,2,64]{2,1,0:T(2,128)(2,1)} %param.18) | copy-start | bytes 43012
  222.2 51.5 %copy-start.57 = (bf16[56,2,64]{2,1,0:T(2,128)(2,1)S(1)}, bf16[56,2,64]{2,1,0:T(2,128)(2,1)}, u32[]{:S(2)}) copy-start(bf16[56,2,64]{2,1,0:T(2,128)(2,1)} %param.19) | copy-start | bytes 43012
  222.2 636.4 %all-gather.8.cloned.1.call-start = ((), (), s32[]{:S(2)}) async-start(), calls=%async_computation.9 | async-start | bytes 3411968 | tf_op jit(solution)/shard_map/all_gather | solution.py:100
  223.0 732.1 %all-gather.10.cloned.1.call-start = ((), (), s32[]{:S(2)}) async-start(), calls=%async_computation.10 | async-start | bytes 1705984 | tf_op jit(solution)/shard_map/all_gather | solution.py:100
  223.5 742.6 %all-gather.14.cloned.1.call-start = ((), (), s32[]{:S(2)}) async-start(), calls=%async_computation.12 | async-start | bytes 9261056 | tf_op jit(solution)/shard_map/all_gather | solution.py:100
  224.1 771.6 %all-gather.12.cloned.1.call-start = ((), (), s32[]{:S(2)}) async-start(), calls=%async_computation.11 | async-start | bytes 9261056 | tf_op jit(solution)/shard_map/all_gather | solution.py:100
  224.7 1214.9 %reduce-scatter.18.cloned.1.call-start = ((), (), s32[]{:S(2)}) async-start(), calls=%async_computation.17 | async-start | bytes 974848 | tf_op jit(solution)/shard_map/reduce_scatter | solution.py:102
  224.8 684.2 %copy-start.17 = (pred[512,512]{0,1:T(8,128)(4,1)}, pred[512,512]{0,1:T(8,128)(4,1)S(1)}, u32[]{:S(2)}) copy-start(pred[512,512]{0,1:T(8,128)(4,1)S(1)} %iota_compare_fusion.1) | copy-start | bytes 786436
  258.8 629.4 %copy-start.47 = (f32[896]{0:T(1024)}, f32[896]{0:T(1024)S(1)}, u32[]{:S(2)}) copy-start(f32[896]{0:T(1024)S(1)} %convert_element_type.168) | copy-start | bytes 10756
  273.3 555.3 %copy-start.29 = (bf16[896,2,64]{2,0,1:T(8,128)(2,1)}, bf16[896,2,64]{2,0,1:T(8,128)(2,1)S(1)}, u32[]{:S(2)}) copy-start(bf16[896,2,64]{2,0,1:T(8,128)(2,1)S(1)} %all_gather.36) | copy-start | bytes 688132
  273.6 592.3 %copy-start.31 = (f32[512,32]{0,1:T(8,128)}, f32[512,32]{0,1:T(8,128)S(1)}, u32[]{:S(2)}) copy-start(f32[512,32]{0,1:T(8,128)S(1)} %get-tuple-element.67) | copy-start | bytes 196612
  273.7 592.3 %copy-start.33 = (f32[512,32]{0,1:T(8,128)}, f32[512,32]{0,1:T(8,128)S(1)}, u32[]{:S(2)}) copy-start(f32[512,32]{0,1:T(8,128)S(1)} %get-tuple-element.68) | copy-start | bytes 196612
  287.4 600.7 %copy-start.27 = (bf16[896,2,64]{2,0,1:T(8,128)(2,1)}, bf16[896,2,64]{2,0,1:T(8,128)(2,1)S(1)}, u32[]{:S(2)}) copy-start(bf16[896,2,64]{2,0,1:T(8,128)(2,1)S(1)} %all_gather.35) | copy-start | bytes 688132
  287.4 818.0 %copy-start.58 = (f32[896]{0:T(1024)}, f32[896]{0:T(1024)S(1)}, u32[]{:S(2)}) copy-start(f32[896]{0:T(1024)S(1)} %convert_element_type.176) | copy-start | bytes 10756
  828.6 59.5 %copy-start.45 = (f32[4,512]{1,0:T(4,128)}, f32[4,512]{1,0:T(4,128)S(1)}, u32[]{:S(2)}) copy-start(f32[4,512]{1,0:T(4,128)S(1)} %fusion.80) | copy-start | bytes 24580
  832.3 34.9 %copy-start.38 = (bf16[4,512,2,32]{1,3,2,0:T(8,128)(2,1)}, bf16[4,512,2,32]{1,3,2,0:T(8,128)(2,1)S(1)}, u32[]{:S(2)}) copy-start(bf16[4,512,2,32]{1,3,2,0:T(8,128)(2,1)S(1)} %get-tuple-element.61) | copy-start | bytes 786436
  832.4 34.9 %copy-start.40 = (bf16[4,512,2,32]{1,3,2,0:T(8,128)(2,1)}, bf16[4,512,2,32]{1,3,2,0:T(8,128)(2,1)S(1)}, u32[]{:S(2)}) copy-start(bf16[4,512,2,32]{1,3,2,0:T(8,128)(2,1)S(1)} %get-tuple-element.62) | copy-start | bytes 786436
  867.3 20.9 copy-start.7
  867.3 20.9 copy-start.9
  867.3 20.8 copy-start
  888.2 20.9 copy-start.35
  889.7 49.1 %copy-start.42 = (bf16[4,512,2,64,1]{1,3,4,2,0:T(8,128)(2,1)}, bf16[4,512,2,64,1]{1,3,4,2,0:T(8,128)(2,1)S(1)}, u32[]{:S(2)}) copy-start(bf16[4,512,2,64,1]{1,3,4,2,0:T(8,128)(2,1)S(1)} %fusion.65) | copy-start | bytes 1572868
  909.1 56.4 %copy-start.25 = (f32[4,2,7,512]{3,2,1,0:T(8,128)}, f32[4,2,7,512]{3,2,1,0:T(8,128)S(1)}, u32[]{:S(2)}) copy-start(f32[4,2,7,512]{3,2,1,0:T(8,128)S(1)} %fusion.15) | copy-start | bytes 344068
  965.4 30.3 %copy-start.54 = (f32[4,512]{1,0:T(4,128)}, f32[4,512]{1,0:T(4,128)S(1)}, u32[]{:S(2)}) copy-start(f32[4,512]{1,0:T(4,128)S(1)} %get-tuple-element.71) | copy-start | bytes 24580
  965.4 140.0 %copy-start.52 = (f32[4,512]{1,0:T(4,128)}, f32[4,512]{1,0:T(4,128)S(1)}, u32[]{:S(2)}) copy-start(f32[4,512]{1,0:T(4,128)S(1)} %fusion.81) | copy-start | bytes 24580
  1047.6 27.9 %copy-start.16 = (bf16[4,512,896]{2,1,0:T(8,128)(2,1)S(1)}, bf16[4,512,896]{2,1,0:T(8,128)(2,1)}, u32[]{:S(2)}) copy-start(bf16[4,512,896]{2,1,0:T(8,128)(2,1)} %get-tuple-element.72) | copy-start | bytes 11010052
  1075.4 29.9 %copy-start.55 = (f32[4,512]{1,0:T(4,128)S(1)}, f32[4,512]{1,0:T(4,128)}, u32[]{:S(2)}) copy-start(f32[4,512]{1,0:T(4,128)} %copy-done.54) | copy-start | bytes 24580
  1075.4 30.0 %copy-start.15 = (bf16[4,512,896]{2,1,0:T(8,128)(2,1)S(1)}, bf16[4,512,896]{2,1,0:T(8,128)(2,1)}, u32[]{:S(2)}) copy-start(bf16[4,512,896]{2,1,0:T(8,128)(2,1)} %param.13) | copy-start | bytes 11010052
  1123.1 15.3 copy-start.1
  1123.1 15.3 copy-start.46
  1123.1 15.3 copy-start.48
  1141.1 36.8 %copy-start.26 = (f32[4,2,7,512]{3,2,1,0:T(8,128)S(1)}, f32[4,2,7,512]{3,2,1,0:T(8,128)}, u32[]{:S(2)}) copy-start(f32[4,2,7,512]{3,2,1,0:T(8,128)} %copy-done.25) | copy-start | bytes 344068
  1141.2 36.8 %copy-start.37 = (pred[512,512]{1,0:T(8,128)(4,1)S(1)}, pred[512,512]{1,0:T(8,128)(4,1)}, u32[]{:S(2)}) copy-start(pred[512,512]{1,0:T(8,128)(4,1)} %iota_compare_fusion) | copy-start | bytes 786436
  1141.2 299.9 %reduce-scatter.16.cloned.1.call-start = ((), (), s32[]{:S(2)}) async-start(), calls=%async_computation.16 | async-start | bytes 974848 | tf_op jit(solution)/shard_map/reduce_scatter | solution.py:102
  1177.9 39.2 %copy-start.8 = (bf16[4,512,14,32]{1,3,2,0:T(8,128)(2,1)S(1)}, bf16[4,512,14,32]{1,3,2,0:T(8,128)(2,1)}, u32[]{:S(2)}) copy-start(bf16[4,512,14,32]{1,3,2,0:T(8,128)(2,1)} %copy-done.7) | copy-start | bytes 5505028
  1177.9 39.2 %copy-start.10 = (bf16[4,512,14,32]{1,3,2,0:T(8,128)(2,1)S(1)}, bf16[4,512,14,32]{1,3,2,0:T(8,128)(2,1)}, u32[]{:S(2)}) copy-start(bf16[4,512,14,32]{1,3,2,0:T(8,128)(2,1)} %copy-done.9) | copy-start | bytes 5505028
  1217.1 13.6 copy-start.32
  1217.1 13.6 copy-start.34
  1217.1 14.8 copy-start.2
  1234.5 208.0 %reduce-scatter.26.cloned.1.call-start = ((), (), s32[]{:S(2)}) async-start(), calls=%async_computation.21 | async-start | bytes 3411968
  1243.4 200.7 %reduce-scatter.14.cloned.1.call-start = ((), (), s32[]{:S(2)}) async-start(), calls=%async_computation.15 | async-start | bytes 6823936 | tf_op jit(solution)/shard_map/reduce_scatter | solution.py:102
  1270.6 341.4 %reduce-scatter.22.cloned.1.call-start = ((), (), s32[]{:S(2)}) async-start(), calls=%async_computation.19 | async-start | bytes 18522112 | tf_op jit(solution)/shard_map/reduce_scatter | solution.py:102
  1296.9 499.4 %reduce-scatter.20.cloned.1.call-start = ((), (), s32[]{:S(2)}) async-start(), calls=%async_computation.18 | async-start | bytes 18522112 | tf_op jit(solution)/shard_map/reduce_scatter | solution.py:102
  1323.3 657.4 %reduce-scatter.24.cloned.1.call-start = ((), (), s32[]{:S(2)}) async-start(), calls=%async_computation.20 | async-start | bytes 18522112 | tf_op jit(solution)/shard_map/reduce_scatter | solution.py:102
  1351.7 843.5 %all-gather.18.cloned.1.call-start = ((), (), s32[]{:S(2)}) async-start(), calls=%async_computation.14 | async-start | bytes 62390272 | tf_op jit(solution)/shard_map/all_gather | solution.py:103
  1356.1 11.6 copy-start.28
  (30 other events, 133.2 us)
Sparse Core Ops, SparseCore 0:
  10.2 52.5 all-gather.15
  222.3 603.3 reduce-scatter.11
  828.0 30.5 all-gather.7
  860.7 26.8 all-gather.9
  889.8 49.7 all-gather.13
  941.6 49.7 all-gather.11
  1141.3 55.2 reduce-scatter.17
  1234.6 55.1 reduce-scatter.15
  1292.2 58.9 reduce-scatter.25
  1353.2 73.5 reduce-scatter.13
  1429.1 182.8 reduce-scatter.21
  1614.2 182.0 reduce-scatter.19
  1798.6 182.0 reduce-scatter.23
  1983.4 211.8 all-gather.17
where the time goes:
time: 2510 us; the launch traced here: 2500 us
  waiting for transfers between devices  1280 us (51%)
  matrix products  461 us (18%)
  other arithmetic  455 us (18%)
  local copies, waits for them, and re-layouts  178 us (7%)
  blocking collectives  109 us (4%)
    reduce_scatter x6, waiting for transfers between devices, device_step(): lax.psum_scatter(part_grad, AXIS_NAME, scatter_dimension=0, tiled=True)  531 us
    reduce_scatter x1, waiting for transfers between devices, device_step(): lax.psum_scatter(part_emb, AXIS_NAME, scatter_dimension=0, tiled=True)  511 us
    scatter-add x1, other arithmetic, device_step(): jax.ops.segment_sum(d_emb_all.reshape(-1, d_emb_all.shape[-1]).astype(jnp...  283 us
    all_gather x1, waiting for transfers between devices, device_step(): d_emb_all = lax.all_gather(d_emb, AXIS_NAME, axis=0, tiled=True)  212 us
    gather x1, local copies, waits for them, and re-layouts, device_step(): picked = jnp.take(table, jnp.where(owned, rel_ids, 0), axis=0)  159 us
    dot_general x3, matrix products, attend(): jnp.einsum('bkgqs,bskd->bqkgd', prob_bf, v_bf16, preferred_element_type=j...  67.5 us
    unnamed x2, blocking collectives  65.6 us
    dot_general x1, matrix products, layer_pass(): jnp.einsum('bsd,df->bsf', h_two, w_gate, preferred_element_type=jnp.float32)  51.9 us
  transfers between devices with their start and end apart: 14, of which 6 were waited for; matrix products, arithmetic and copies ran while one was open for 26% of the time, Pallas kernels for 0%

commit v1 on v0

v1 whole, which is shorter than its diff:
```python
import jax
import jax.numpy as jnp
from jax import lax
from jax.sharding import PartitionSpec as P

AXIS_NAME = "fsdp"
NORM_EPS = 1e-5
ROPE_THETA = 500000.0
N_DEV = 16
SLOTS = 128
RING = (0, 1, 2, 3, 6, 7, 4, 5, 12, 13, 14, 15, 10, 11, 8, 9)
F32 = jnp.float32
BF16 = jnp.bfloat16


def rms_norm(x_f32, gain_f32):
    inv_rms = lax.rsqrt(jnp.mean(x_f32 * x_f32, axis=-1, keepdims=True) + NORM_EPS)
    return (x_f32 * inv_rms * gain_f32).astype(BF16)


def rotary(x_f32):
    head_dim = x_f32.shape[-1]
    half_dim = head_dim // 2
    seq_len = x_f32.shape[-3]
    inv_freq = ROPE_THETA ** (-2.0 * jnp.arange(half_dim, dtype=F32) / head_dim)
    angles = jnp.arange(seq_len, dtype=F32)[:, None] * inv_freq[None, :]
    cos_tab = jnp.cos(angles)[:, None, :]
    sin_tab = jnp.sin(angles)[:, None, :]
    lo_half = x_f32[..., :half_dim]
    hi_half = x_f32[..., half_dim:]
    return jnp.concatenate([lo_half * cos_tab - hi_half * sin_tab, hi_half * cos_tab + lo_half * sin_tab], axis=-1)


def attend(q_f32, k_f32, v_bf16):
    batch_loc, seq_len, q_heads, head_dim = q_f32.shape
    kv_heads = k_f32.shape[2]
    q_rot = rotary(q_f32).astype(BF16).reshape(batch_loc, seq_len, kv_heads, q_heads // kv_heads, head_dim)
    k_rot = rotary(k_f32).astype(BF16)
    scores = jnp.einsum("bqkgd,bskd->bkgqs", q_rot, k_rot, preferred_element_type=F32) * head_dim ** -0.5
    positions = jnp.arange(seq_len)
    causal = positions[:, None] >= positions[None, :]
    scores = jnp.where(causal, scores, -1e30)
    prob_bf = jax.nn.softmax(scores, axis=-1).astype(BF16)
    attn_out = jnp.einsum("bkgqs,bskd->bqkgd", prob_bf, v_bf16, preferred_element_type=F32)
    return attn_out.astype(BF16).reshape(batch_loc, seq_len, q_heads * head_dim)


def gated(gate_f32, up_f32):
    return (jax.nn.silu(gate_f32) * up_f32).astype(BF16)


def mm(a, b):
    return jnp.dot(a, b, preferred_element_type=F32)


def mm_tn(a, b):
    return lax.dot_general(a, b, (((0,), (0,)), ((), ())), preferred_element_type=F32)


def mm_nt(a, b):
    return lax.dot_general(a, b, (((1,), (1,)), ((), ())), preferred_element_type=F32)


def ring_scatter(partial):
    return lax.psum_scatter(partial, AXIS_NAME, scatter_dimension=0, tiled=True, axis_index_groups=[list(RING)])


def to_owner(ring_block):
    return lax.ppermute(ring_block.astype(BF16), AXIS_NAME, [(RING[j], j) for j in range(N_DEV)])


def to_all(mine):
    copies = jnp.broadcast_to(mine[None], (N_DEV,) + mine.shape).reshape((-1,) + mine.shape[1:])
    return lax.all_to_all(copies, AXIS_NAME, 0, 0, tiled=True)


def plan_requests(ids, rows_dev):
    n_tok = ids.shape[0]
    owner = ids // rows_dev
    pos = jnp.arange(n_tok, dtype=jnp.int32)
    first = jnp.min(jnp.where(ids[:, None] == ids[None, :], pos[None, :], n_tok), axis=1)
    lead_owner = jnp.where(first == pos, owner, -1)
    rank = jnp.sum((lead_owner[None, :] == owner[:, None]) & (pos[None, :] < first[:, None]), axis=1, dtype=jnp.int32)
    slot = jnp.where(rank < SLOTS, owner * SLOTS + rank, N_DEV * SLOTS)
    lead_slot = jnp.where(first == pos, slot, N_DEV * SLOTS)
    local_row = ids - owner * rows_dev
    slots = jnp.arange(N_DEV * SLOTS, dtype=jnp.int32)
    asked = jnp.sum(jnp.where(lead_slot[None, :] == slots[:, None], local_row[None, :], 0), axis=1, dtype=jnp.int32)
    spill = jnp.any(rank >= SLOTS).astype(jnp.int32)
    return slot, asked, spill


def solution(mesh):
    spec_1d = P(AXIS_NAME)
    spec_2d = P(AXIS_NAME, None)
    spec_3d = P(AXIS_NAME, None, None)
    in_specs = (spec_2d, spec_3d, spec_2d, spec_1d, spec_1d, spec_3d, spec_3d, spec_3d, spec_2d, spec_2d, spec_2d, spec_2d)
    out_specs = (spec_3d, spec_2d, spec_1d, spec_1d, spec_3d, spec_3d, spec_3d, spec_2d, spec_2d, spec_2d, spec_2d)

    def device_step(token_ids, grad_y, table, norm1, norm2, w_query, w_key, w_value, w_out, w_gate, w_up, w_down):
        batch_loc, seq_len = token_ids.shape
        rows_dev, dim = table.shape
        n_tok = batch_loc * seq_len
        q_heads, head_dim = w_query.shape[1:]
        kv_heads = w_key.shape[1]
        ffn = w_gate.shape[1]
        shard = w_query.shape[0]
        q_w, kv_w = q_heads * head_dim, kv_heads * head_dim
        me = lax.axis_index(AXIS_NAME)

        ids = token_ids.reshape(n_tok)
        slot, asked, spill = plan_requests(ids, rows_dev)
        ask_row = jnp.concatenate([asked.reshape(N_DEV, SLOTS), jnp.full((1, SLOTS), spill, jnp.int32)], axis=0)
        ask_all = lax.all_gather(ask_row, AXIS_NAME, axis=0)
        asked_of_me = lax.dynamic_index_in_dim(ask_all, me, axis=1, keepdims=False).reshape(N_DEV * SLOTS)
        any_spill = jnp.max(ask_all[:, N_DEV, 0]) > 0

        gains_col = jnp.pad(jnp.stack([norm1, norm2], axis=1), ((0, 0), (0, 126)))
        pack_a = jnp.concatenate([w_query.reshape(shard, q_w), w_key.reshape(shard, kv_w), w_value.reshape(shard, kv_w), gains_col], axis=1)
        pack_b = jnp.concatenate([w_gate, w_up], axis=1)
        w_a = lax.all_gather(pack_a, AXIS_NAME, axis=0, tiled=True)
        w_o = lax.all_gather(w_out, AXIS_NAME, axis=0, tiled=True)
        w_d = lax.all_gather(w_down, AXIS_NAME, axis=0, tiled=True)
        w_gu = lax.all_gather(pack_b, AXIS_NAME, axis=0, tiled=True)
        w_qkv = w_a[:, : q_w + 2 * kv_w]
        gain_one = w_a[:, q_w + 2 * kv_w].astype(F32)
        gain_two = w_a[:, q_w + 2 * kv_w + 1].astype(F32)

        sent_rows = jnp.take(table, asked_of_me, axis=0)
        got_rows = lax.all_to_all(sent_rows, AXIS_NAME, 0, 0, tiled=True)

        def rows_short(args):
            return jnp.take(args[0], jnp.minimum(args[1], N_DEV * SLOTS - 1), axis=0)

        def rows_dense(args):
            ids_all = to_all(args[2])
            rel_ids = ids_all - me * rows_dev
            owned = (rel_ids >= 0) & (rel_ids < rows_dev)
            picked = jnp.take(args[3], jnp.where(owned, rel_ids, 0), axis=0)
            part = jnp.where(owned[:, None], picked, jnp.zeros((), BF16))
            parts = lax.all_to_all(part, AXIS_NAME, 0, 0, tiled=True).reshape(N_DEV, n_tok, dim)
            return jnp.sum(parts.astype(F32), axis=0).astype(BF16)

        x_bf = lax.cond(any_spill, rows_dense, rows_short, (got_rows, slot, ids, table))

        dy = grad_y.reshape(n_tok, dim)
        x_f32 = x_bf.astype(F32)
        h_one, norm1_pull = jax.vjp(rms_norm, x_f32, gain_one)
        qkv = mm(h_one, w_qkv)
        q_f32 = qkv[:, :q_w].reshape(batch_loc, seq_len, q_heads, head_dim)
        k_f32 = qkv[:, q_w : q_w + kv_w].reshape(batch_loc, seq_len, kv_heads, head_dim)
        v_bf16 = qkv[:, q_w + kv_w :].astype(BF16).reshape(batch_loc, seq_len, kv_heads, head_dim)
        attn_out, attn_pull = jax.vjp(attend, q_f32, k_f32, v_bf16)
        attn_flat = attn_out.reshape(n_tok, q_w)
        resid_two = (x_f32 + mm(attn_flat, w_o)).astype(BF16).astype(F32)
        h_two, norm2_pull = jax.vjp(rms_norm, resid_two, gain_two)
        gate_f32 = mm(h_two, w_gu[:, :ffn])
        up_f32 = mm(h_two, w_gu[:, ffn:])
        act_bf16, act_pull = jax.vjp(gated, gate_f32, up_f32)
        layer_out = (resid_two + mm(act_bf16, w_d)).astype(BF16)

        g_down = mm_tn(act_bf16, dy)
        d_act = mm_nt(dy, w_d).astype(BF16)
        d_gate, d_up = act_pull(d_act)
        d_gu = jnp.concatenate([d_gate.astype(BF16), d_up.astype(BF16)], axis=1)
        g_gu = mm_tn(h_two, d_gu)
        g_down, g_gu, d_gu = lax.optimization_barrier((g_down, g_gu, d_gu))
        sum_down = ring_scatter(g_down)
        sum_gu = ring_scatter(g_gu)
        d_h_two = mm_nt(d_gu, w_gu).astype(BF16)
        d_resid_two, g_norm2 = norm2_pull(d_h_two)
        d_resid = (dy.astype(F32) + d_resid_two).astype(BF16)
        g_out = mm_tn(attn_flat, d_resid)
        d_attn = mm_nt(d_resid, w_o).astype(BF16)
        d_query, d_key, d_value = attn_pull(d_attn.reshape(batch_loc, seq_len, q_w))
        d_qkv = jnp.concatenate([d_query.astype(BF16).reshape(n_tok, q_w), d_key.astype(BF16).reshape(n_tok, kv_w), d_value.reshape(n_tok, kv_w)], axis=1)
        g_qkv = mm_tn(h_one, d_qkv)
        d_h_one = mm_nt(d_qkv, w_qkv).astype(BF16)
        d_x, g_norm1 = norm1_pull(d_h_one)
        d_emb = (d_resid.astype(F32) + d_x).astype(BF16)
        g_norms = jnp.pad(jnp.stack([g_norm1, g_norm2], axis=1), ((0, 0), (0, 126)))

        chosen = (slot[:, None] == jnp.arange(N_DEV * SLOTS, dtype=jnp.int32)[None, :]).astype(BF16)
        slot_sums = mm_tn(chosen, d_emb)
        got_sums = lax.all_to_all(slot_sums, AXIS_NAME, 0, 0, tiled=True)
        g_rest = jnp.concatenate([g_qkv, g_norms, g_out], axis=1)
        g_rest, sum_down, sum_gu, got_sums = lax.optimization_barrier((g_rest, sum_down, sum_gu, got_sums))
        out_down, out_gu, out_rest = to_owner(sum_down), to_owner(sum_gu), to_owner(ring_scatter(g_rest))

        def table_short(args):
            acc = jnp.zeros((rows_dev, dim), F32).at[args[1]].add(args[0])
            return acc.astype(BF16)

        def table_dense(args):
            ids_all = to_all(args[2])
            rel_ids = ids_all - me * rows_dev
            owned = (rel_ids >= 0) & (rel_ids < rows_dev)
            d_all = to_all(args[3])
            seg_ids = jnp.where(owned, rel_ids, rows_dev)
            return jax.ops.segment_sum(d_all.astype(F32), seg_ids, num_segments=rows_dev).astype(BF16)

        d_table = lax.cond(any_spill, table_dense, table_short, (got_sums, asked_of_me, ids, d_emb))

        n_qkv = q_w + 2 * kv_w
        return (
            layer_out.reshape(batch_loc, seq_len, dim),
            d_table,
            out_rest[:, n_qkv],
            out_rest[:, n_qkv + 1],
            out_rest[:, :q_w].reshape(shard, q_heads, head_dim),
            out_rest[:, q_w : q_w + kv_w].reshape(shard, kv_heads, head_dim),
            out_rest[:, q_w + kv_w : n_qkv].reshape(shard, kv_heads, head_dim),
            out_rest[:, n_qkv + 128 :],
            out_gu[:, :ffn],
            out_gu[:, ffn:],
            out_down,
        )

    return jax.shard_map(device_step, mesh=mesh, in_specs=in_specs, out_specs=out_specs, check_vma=False)
```

time: 2510 us -> 1000 us (0.40)
  waiting for transfers between devices: 1280 us -> 152 us
  other arithmetic: 455 us -> 222 us
  blocking collectives: 109 us -> 15.3 us
  local copies, waits for them, and re-layouts: 178 us -> 123 us
    reduce_scatter x7 -> x2, waiting for transfers between devices: 1040 us -> 1.94 us  [ring_scatter(): lax.psum_scatter(partial, AXIS_NAME, scatter_dimension=0, tiled=True, axi...]
    scatter-add x1, other arithmetic: 283 us -> 32.2 us  [table_short(): acc = jnp.zeros((rows_dev, dim), F32).at[args[1]].add(args[0])]
    all_gather x6 -> x4, waiting for transfers between devices: 239 us -> 0.02 us  [the longest x1 0.01 us: device_step(): w_a = lax.all_gather(pack_a, AXIS_NAME, axis=0, tiled=True)]
    all_to_all x0 -> x2, waiting for transfers between devices: none -> 144 us  [the longest x1 96.2 us: device_step(): got_sums = lax.all_to_all(slot_sums, AXIS_NAME, 0, 0, tiled=True)]
    gather x1 -> x2, local copies, waits for them, and re-layouts: 159 us -> 31.3 us  [the longest x1 18.4 us: device_step(): sent_rows = jnp.take(table, asked_of_me, axis=0)]
    unnamed x2 -> x0, blocking collectives: 65.6 us -> none
    select_n x1 -> x5, other arithmetic: 39.3 us -> 4.29 us  [the longest x2 3.66 us: device_step(): sent_rows = jnp.take(table, asked_of_me, axis=0)]
    concatenate x0 -> x4, other arithmetic: none -> 33.7 us  [the longest x1 27 us: device_step(): d_gu = jnp.concatenate([d_gate.astype(BF16), d_up.astype(BF16)], axis=1)]
  transfers between devices with their start and end apart: 14 -> 12, of which waited for: 6 -> 4; matrix products, arithmetic and copies ran while one was open for 26% -> 59% of each run, Pallas kernels for 0% -> 0%
where the time goes in v1:
time: 1000 us; the launch traced here: 984 us
  matrix products  444 us (44%)
  other arithmetic  222 us (22%)
  waiting for transfers between devices  152 us (15%)
  local copies, waits for them, and re-layouts  123 us (12%)
  between operations  16.5 us (2%)
  blocking collectives  15.3 us (2%)
    dot_general x5, matrix products, mm(): return jnp.dot(a, b, preferred_element_type=F32)  129 us
    dot_general x5, matrix products, mm_tn(): lax.dot_general(a, b, (((0,), (0,)), ((), ())), preferred_element_type=F32)  105 us
    dot_general x4, matrix products, mm_nt(): lax.dot_general(a, b, (((1,), (1,)), ((), ())), preferred_element_type=F32)  97.3 us
    all_to_all x1, waiting for transfers between devices, device_step(): got_sums = lax.all_to_all(slot_sums, AXIS_NAME, 0, 0, tiled=True)  96.2 us
    dot_general x3, matrix products, attend(): jnp.einsum('bkgqs,bskd->bqkgd', prob_bf, v_bf16, preferred_element_type=F32)  65.2 us
    all_to_all x1, waiting for transfers between devices, device_step(): got_rows = lax.all_to_all(sent_rows, AXIS_NAME, 0, 0, tiled=True)  47.5 us
    dot_general x3, matrix products, attend(): jnp.einsum('bqkgd,bskd->bkgqs', q_rot, k_rot, preferred_element_type=F32)  47.1 us
    mul x1, other arithmetic, attend(): jnp.einsum('bqkgd,bskd->bkgqs', q_rot, k_rot, preferred_element_type=F32)  39.4 us
  transfers between devices with their start and end apart: 12, of which 4 were waited for; matrix products, arithmetic and copies ran while one was open for 59% of the time, Pallas kernels for 0%

profile of v1, /device:TPU:0, one launch (start us, length us, event | category | flops | bytes accessed | tf_op | source)
XLA Modules:
  0.0 983.5 jit_solution(3397636184250593512)
XLA Ops:
  18.9 4.1 convert_reduce_fusion
  26.6 15.3 %all-gather.1 = s32[16,17,128]{2,1,0:T(8,128)S(1)} all-gather(s32[1,17,128]{2,1,0:T(8,128)S(1)} %pad_bitcast_fusion), channel_id=2, replica_groups=mesh['fsdp'=16] {'fsdp'}, dimensions={0}, use_global_device_ids=true | all-gather | bytes 147968 | tf_op jit(solution)/shard_map/all_gather | solution.py:114
  42.0 18.4 %gather_fusion.2 = bf16[2048,896]{1,0:T(8,128)(2,1)} fusion(bf16[9496,896]{1,0:T(8,128)(2,1)} %param.18, s32[2048]{0:T(1024)S(1)} %broadcast_clamp_fusion.2), kind=kCustom, calls=%fused_computation.2 | custom fusion | bytes 7348224 | tf_op jit(solution)/shard_map/jit(_take)/gather | solution.py:129
  70.5 47.5 %all-to-all-done.4 = bf16[16,128,896]{2,1,0:T(8,128)(2,1)} async-done(((bf16[16,128,896]{2,1,0:T(8,128)(2,1)}), bf16[16,128,896]{2,1,0:T(8,128)(2,1)}, u32[]{:S(2)}, u32[]{:S(2)}) %all-to-all-start.4) | async-done | bytes 3670048 | tf_op jit(solution)/shard_map/all_to_all | solution.py:130
  118.0 26.6 %conditional.7 = (f32[2048,896]{1,0:T(8,128)}, f32[2048,896]{1,0:T(8,128)}, f32[2048]{0:T(1024)}, f32[2048]{0:T(1024)S(1)}) conditional(s32[]{:T(128)} %convert_element_type.193, (s32[2048]{0:T(1024)S(1)}, s32[2048]{0:T(1024)S(1)}, s32[2048]{0:T(1024)S(1)}, s32[2048]{0:T(1024)S(1)}, s32[2048]{0:T(1024)S(1)}, ...), branch_computations={%region_5.7_spmd, %region_7.10_spmd} | conditional | flops 92370944 | bytes 442155104 | solution.py:144
  118.2 12.9 %gather_fusion = bf16[2048,896]{1,0:T(8,128)(2,1)} fusion(bf16[2048,896]{1,0:T(8,128)(2,1)} %bitcast, s32[2048]{0:T(1024)S(1)} %broadcast_clamp_fusion), kind=kCustom, calls=%fused_computation | custom fusion | bytes 7348224 | tf_op jit(solution)/shard_map/cond/branch_0_fun/jit(_take)/gather | solution.py:133
  131.1 5.9 multiply_reduce_fusion
  137.0 6.5 copy.182
  147.2 8.6 fusion.55
  162.5 8.6 copy.95
  171.1 10.0 %reshape.459 = f32[4,512,14,64]{1,0,3,2:T(4,128)} reshape(f32[2048,896]{0,1:T(8,128)} %copy.95) | data formatting | bytes 14680064 | tf_op jit(solution)/shard_map/reshape | solution.py:150
  181.1 4.3 subtract_convert_fusion
  190.0 4.3 fusion.88
  204.7 22.3 %fusion.18 = (f32[4,2,7,512]{3,2,1,0:T(8,128)S(1)}, f32[4,2,512,512,7]{3,2,4,1,0:T(8,128)}) fusion(pred[512,512]{0,1:T(8,128)(4,1)S(1)} %copy-done.10, bf16[4,512,2,7,32]{1,4,3,2,0:T(8,128)(2,1)S(1)} %bitcast.173, bf16[4,512,2,7,32]{1,4,3,2,0:T(8,128)(2,1)} %bitcast.175, bf16[4,512,2,32]{1,3,2,0:T(8,128)(2,1)S(1)} %get-tuple-element.193, ...), kind=kOutput, calls=%fused_computation.51 | convolution fusion | flops 1931448320 | bytes 63291392 | tf_op jit(solution)/shard_map/jvp(bqkgd,bskd->bkgqs)/dot_general | solution.py:39
  227.0 19.2 %fusion.24 = f32[4,2,7,512]{3,2,1,0:T(8,128)S(1)} fusion(f32[4,2,512,512,7]{3,2,4,1,0:T(8,128)} %get-tuple-element.206, f32[4,2,7,512]{3,2,1,0:T(8,128)S(1)} %get-tuple-element.205, pred[512,512]{0,1:T(8,128)(4,1)S(1)} %copy-done.10), kind=kLoop, calls=%fused_computation.62 | loop fusion | flops 58691584 | bytes 59211776 | tf_op jit(solution)/shard_map/jvp()/reduce_sum | solution.py:43
  246.3 29.9 %divide_convert_fusion = bf16[4,2,7,512,512]{3,4,2,1,0:T(8,128)(2,1)} fusion(f32[4,2,512,512,7]{3,2,4,1,0:T(8,128)} %get-tuple-element.206, f32[4,2,7,512]{3,2,1,0:T(8,128)S(1)} %fusion.24, f32[4,2,7,512]{3,2,1,0:T(8,128)S(1)} %get-tuple-element.205, pred[512,512]{0,1:T(8,128)(4,1)S(1)} %copy-done.10), kind=kLoop, calls=%fused_computation.49 | loop fusion | flops 73400320 | bytes 88571904 | tf_op jit(solution)/shard_map/jvp()/convert_element_type | solution.py:43
  276.2 14.4 %convert_bitcast_fusion.1 = bf16[4,512,2,7,64]{1,4,3,2,0:T(8,128)(2,1)S(1)} fusion(bf16[4,2,7,512,512]{3,4,2,1,0:T(8,128)(2,1)} %divide_convert_fusion, bf16[4,512,2,64,1]{1,0,3,2,4:T(4,128)(2,1)S(1)} %bitcast.183), kind=kOutput, calls=%fused_computation.116 | convolution fusion | flops 1880883200 | bytes 33554432 | tf_op jit(solution)/shard_map/jvp(bkgqs,bskd->bqkgd)/dot_general | solution.py:44
  296.7 11.5 %fusion.46 = (f32[2048]{0:T(1024)S(1)}, bf16[2048,896]{1,0:T(8,128)(2,1)}) fusion(f32[2048,896]{1,0:T(8,128)} %get-tuple-element.104, bf16[2048,896]{0,1:T(8,128)(2,1)} %bitcast.177, bf16[896,896]{1,0:T(8,128)(2,1)} %all-gather.9.cloned.1.call-done), kind=kOutput, calls=%fused_computation.106 | convolution fusion | flops 3297507328 | bytes 16293888 | tf_op jit(solution)/shard_map/dot_general | solution.py:53
  308.8 28.1 %convolution_convert_fusion.1 = bf16[2048,4864]{1,0:T(8,128)(2,1)} fusion(bf16[2048,896]{1,0:T(8,128)(2,1)} %bitcast.179, bf16[4864,896]{1,0:T(8,128)(2,1)} %all-gather.13.cloned.1.call-done), kind=kOutput, calls=%fused_computation.64 | convolution fusion | flops 17860919296 | bytes 32309248 | tf_op jit(solution)/shard_map/dot_general | solution.py:61
  336.8 29.4 %fusion.31 = f32[2048,4864]{1,0:T(8,128)} fusion(bf16[896,9728]{1,0:T(8,128)(2,1)} %all-gather.11.cloned.1.call-done, bf16[2048,896]{1,0:T(8,128)(2,1)} %get-tuple-element.208, f32[896]{0:T(1024)S(1)} %get-tuple-element.161, f32[2048]{0:T(1024)S(1)} %fusion.78), kind=kOutput, calls=%fused_computation.90 | convolution fusion | flops 17858297856 | bytes 52243968 | tf_op jit(solution)/shard_map/dot_general | solution.py:53
  366.3 52.5 %fusion.22 = (bf16[2048,4864]{1,0:T(8,128)(2,1)}, bf16[2048,4864]{1,0:T(8,128)(2,1)}, bf16[2048,4864]{1,0:T(8,128)(2,1)}) fusion(f32[2048,4864]{1,0:T(8,128)} %fusion.31, bf16[2048,4864]{1,0:T(8,128)(2,1)} %convolution_convert_fusion.1, bf16[896,9728]{1,0:T(8,128)(2,1)} %all-gather.11.cloned.1.call-done, bf16[2048,896]{1,0:T(8,128)(2,1)} %get-tuple-element.208, ...), kind=kOutput, calls=%fused_computation.57 | convolution fusion | flops 18027642880 | bytes 131935744 | tf_op jit(solution)/shard_map/dot_general | solution.py:53
  418.7 49.4 %fusion.83 = f32[896,9728]{1,0:T(8,128)} fusion(bf16[2048,896]{1,0:T(8,128)(2,1)} %get-tuple-element.208, f32[896]{0:T(1024)S(1)} %get-tuple-element.161, f32[2048]{0:T(1024)S(1)} %fusion.78, bf16[2048,4864]{1,0:T(8,128)(2,1)} %get-tuple-element.181, bf16[2048,4864]{1,0:T(8,128)(2,1)} %get-tuple-element.179), kind=kOutput, calls=%fused_computation.196 | convolution fusion | flops 35788947456 | bytes 78392832 | tf_op jit(solution)/shard_map/dot_general | solution.py:57
  468.2 27.0 %pad_maximum_fusion = bf16[2048,9728]{1,0:T(8,128)(2,1)} fusion(bf16[2048,4864]{1,0:T(8,128)(2,1)} %get-tuple-element.181, bf16[2048,4864]{1,0:T(8,128)(2,1)} %get-tuple-element.179), kind=kLoop, calls=%fused_computation.58 | loop fusion | flops 79691776 | bytes 79691776 | tf_op jit(solution)/shard_map/concatenate | solution.py:165
  495.1 28.4 %fusion.92 = f32[4864,896]{1,0:T(8,128)} fusion(bf16[2048,4864]{1,0:T(8,128)(2,1)} %get-tuple-element.180, bf16[2048,896]{1,0:T(8,128)(2,1)} %bitcast.180), kind=kOutput, calls=%fused_computation.202 | convolution fusion | flops 17850957824 | bytes 41025536 | tf_op jit(solution)/shard_map/dot_general | solution.py:57
  524.5 53.0 %fusion.48 = (f32[2048]{0:T(1024)S(1)}, f32[896]{0:T(1024)}, bf16[2048,896]{1,0:T(8,128)(2,1)}) fusion(bf16[2048,896]{1,0:T(8,128)(2,1)} %get-tuple-element.208, f32[896]{0:T(1024)S(1)} %get-tuple-element.161, f32[2048]{0:T(1024)S(1)} %fusion.78, bf16[2048,9728]{1,0:T(8,128)(2,1)} %pad_maximum_fusion, bf16[896,9728]{1,0:T(8,128)(2,1)} %all-gather.11.cloned.1.call-done), kind=kOutput, calls=%fused_computation.108 | convolution fusion | flops 35718430720 | bytes 64642048 | tf_op jit(solution)/shard_map/dot_general | solution.py:61
  577.6 4.6 fusion.43
  584.1 5.8 convolution_convert_fusion.4
  589.9 6.2 copy.101
  596.1 7.2 reshape_reshape.3
  603.3 37.2 %fusion.17 = (f32[4,2,7,512]{3,2,1,0:T(8,128)S(1)}, bf16[4,2,7,512,512]{3,4,2,1,0:T(8,128)(2,1)}) fusion(f32[4,2,512,512,7]{3,2,4,1,0:T(8,128)} %get-tuple-element.206, f32[4,2,7,512]{3,2,1,0:T(8,128)S(1)} %multiply_divide_fusion, f32[4,2,7,512]{3,2,1,0:T(8,128)S(1)} %copy-done.23, pred[512,512]{0,1:T(8,128)(4,1)S(1)} %copy-done.11, ...), kind=kOutput, calls=%fused_computation.47 | convolution fusion | flops 1996460032 | bytes 92880896 | tf_op jit(solution)/shard_map/transpose(jvp(bkgqs,bskd->bqkgd))/dot_general | solution.py:44
  640.5 39.4 %fusion.15 = bf16[4,2,512,512,7]{3,2,4,1,0:T(8,128)(2,1)} fusion(bf16[4,2,7,512,512]{3,4,2,1,0:T(8,128)(2,1)} %get-tuple-element.211, f32[4,2,512,512,7]{3,2,4,1,0:T(8,128)} %get-tuple-element.206, f32[4,2,512,7]{2,3,1,0:T(8,128)S(1)} %bitcast.192, f32[4,2,512,7]{2,3,1,0:T(8,128)S(1)} %negate_bitcast_fusion, f32[4,2,512,7]{2,3,1,0:T(8,128)S(1)} %bitcast.189, ...), kind=kLoop, calls=%fused_computation.45 | loop fusion | flops 146800640 | bytes 118046720 | tf_op jit(solution)/shard_map/transpose(jvp())/mul | solution.py:39
  680.0 11.3 %convert_convert_fusion = f32[4,2,512,7,64]{2,4,3,1,0:T(8,128)S(1)} fusion(bf16[4,2,512,512,7]{3,2,4,1,0:T(8,128)(2,1)} %fusion.15, bf16[4,512,2,32]{1,3,2,0:T(8,128)(2,1)S(1)} %copy-done.27, bf16[4,512,2,32]{1,3,2,0:T(8,128)(2,1)S(1)} %copy-done.25), kind=kOutput, calls=%fused_computation.115 | convolution fusion | flops 1881931776 | bytes 37224448 | tf_op jit(solution)/shard_map/transpose(jvp(bqkgd,bskd->bkgqs))/dot_general | solution.py:39
  692.6 7.6 multiply_add_fusion.1
  703.8 13.5 %fusion.66 = f32[4,512,2,64]{1,3,2,0:T(8,128)S(1)} fusion(bf16[4,2,512,512,7]{3,2,4,1,0:T(8,128)(2,1)} %fusion.15, bf16[4,512,2,7,32]{1,4,3,2,0:T(8,128)(2,1)S(1)} %bitcast.174, bf16[4,512,2,7,32]{1,4,3,2,0:T(8,128)(2,1)S(1)} %bitcast.176), kind=kOutput, calls=%fused_computation.136 | convolution fusion | flops 1886650368 | bytes 34078720 | tf_op jit(solution)/shard_map/transpose(jvp(bqkgd,bskd->bkgqs))/dot_general | solution.py:39
  719.3 13.5 %fusion.67 = bf16[4,512,2,64]{1,3,2,0:T(8,128)(2,1)S(1)} fusion(bf16[4,2,7,512,512]{3,4,2,1,0:T(8,128)(2,1)} %divide_convert_fusion, bf16[4,2,64,7,512]{4,0,2,3,1:T(4,128)(2,1)S(1)} %bitcast.170), kind=kOutput, calls=%fused_computation.137 | convolution fusion | flops 1879310336 | bytes 33554432 | tf_op jit(solution)/shard_map/transpose(jvp(bkgqs,bskd->bqkgd))/dot_general | solution.py:44
  734.5 10.4 %fusion.39 = (f32[2048]{0:T(1024)S(1)}, f32[896]{0:T(1024)S(1)}, bf16[2048,896]{1,0:T(8,128)(2,1)S(1)}) fusion(f32[2048,896]{1,0:T(8,128)} %get-tuple-element.104, f32[896]{0:T(1024)S(1)} %copy-done.40, f32[2048]{0:T(1024)S(1)} %copy-done.36, bf16[2048,1152]{0,1:T(8,128)(2,1)S(1)} %constant_dynamic-update-slice_fusion, bf16[896,1280]{1,0:T(8,128)(2,1)S(1)} %copy-done.28), kind=kOutput, calls=%fused_computation.99 | convolution fusion | flops 4242535424 | bytes 17817088 | tf_op jit(solution)/shard_map/dot_general | solution.py:61
  745.0 4.3 fusion.45
  749.4 11.5 %fusion.26 = f32[2048,896]{1,0:T(8,128)} fusion(bf16[2048,896]{1,0:T(8,128)(2,1)S(1)} %fusion.45, s32[2048]{0:T(1024)S(1)} %copy-done.41), kind=kOutput, calls=%fused_computation.72 | convolution fusion | flops 7520387072 | bytes 11018240 | tf_op jit(solution)/shard_map/dot_general | solution.py:57
  760.9 3.8 all-to-all-start.5
  765.0 7.2 fusion.93
  772.3 8.4 fusion.82
  780.7 3.8 fusion.36
  784.5 96.2 %all-to-all-done.5 = f32[16,128,896]{2,1,0:T(8,128)} async-done(((f32[16,128,896]{2,1,0:T(8,128)}), f32[16,128,896]{2,1,0:T(8,128)}, u32[]{:S(2)}, u32[]{:S(2)}) %all-to-all-start.5) | async-done | bytes 7340064 | tf_op jit(solution)/shard_map/all_to_all | solution.py:185
  887.2 27.5 %fusion.47 = bf16[2048,896]{1,0:T(8,128)(2,1)} fusion(bf16[2048,896]{1,0:T(8,128)(2,1)} %get-tuple-element.208, bf16[2048,4864]{1,0:T(8,128)(2,1)} %get-tuple-element.180, bf16[4864,896]{1,0:T(8,128)(2,1)} %all-gather.13.cloned.1.call-done), kind=kOutput, calls=%fused_computation.107 | convolution fusion | flops 17856462848 | bytes 35979264 | tf_op jit(solution)/shard_map/dot_general | solution.py:53
  914.7 49.8 %conditional.8 = (bf16[9496,896]{1,0:T(8,128)(2,1)}) conditional(s32[]{:T(128)} %convert_element_type.193, (s32[16,1,128]{2,1,0:T(1,128)S(1)}, f32[2048,896]{1,0:T(8,128)}) %tuple.113, (s32[4,512]{1,0:T(4,128)S(1)}, s32[]{:T(128)}, bf16[2048,896]{1,0:T(8,128)(2,1)}) %tuple.115), branch_computations={%region_20.22_spmd, %region_22.24_spmd} | conditional | flops 67392512 | bytes 383297600
  914.7 32.2 %scatter_custom_fusion = f32[9496,896]{1,0:T(8,128)} fusion(s32[2048]{0:T(1024)S(1)} %bitcast.209, f32[2048,896]{1,0:T(8,128)} %get-tuple-element.80, f32[]{:T(128)} %constant.68.clone), kind=kCustom, calls=%fused_computation.30 | custom fusion | flops 1835008 | bytes 34034176 | tf_op jit(solution)/shard_map/cond/branch_0_fun/scatter-add | solution.py:191
  947.0 17.4 %convert_element_type.140 = bf16[9496,896]{1,0:T(8,128)(2,1)} convert(f32[9496,896]{1,0:T(8,128)} %scatter_custom_fusion) | non-fusion elementwise | flops 8508416 | bytes 51050496 | tf_op jit(solution)/shard_map/cond/branch_0_fun/convert_element_type | solution.py:192
  964.5 4.7 reduce-scatter.11.cloned.1.call-done
  (199 shorter events, 81.0 us)
Async XLA Ops:
  7.2 138.0 %all-gather.7.cloned.1.call-start = ((), (), s32[]{:S(2)}) async-start(), calls=%async_computation.9 | async-start | bytes 2437120 | tf_op jit(solution)/shard_map/all_gather | solution.py:121
  11.5 285.1 %all-gather.9.cloned.1.call-start = ((), (), s32[]{:S(2)}) async-start(), calls=%async_computation.10 | async-start | bytes 1705984 | tf_op jit(solution)/shard_map/all_gather | solution.py:122
  12.3 296.5 %all-gather.13.cloned.1.call-start = ((), (), s32[]{:S(2)}) async-start(), calls=%async_computation.12 | async-start | bytes 9261056 | tf_op jit(solution)/shard_map/all_gather | solution.py:123
  13.0 323.8 %all-gather.11.cloned.1.call-start = ((), (), s32[]{:S(2)}) async-start(), calls=%async_computation.11 | async-start | bytes 18522112 | tf_op jit(solution)/shard_map/all_gather | solution.py:124
  42.0 18.5 %copy-start.29 = (s32[16,1,128]{2,1,0:T(1,128)}, s32[16,1,128]{2,1,0:T(1,128)S(1)}, u32[]{:S(2)}) copy-start(s32[16,1,128]{2,1,0:T(1,128)S(1)} %get-tuple-element.172) | copy-start | bytes 24580
  60.4 57.6 %copy-start.33 = (s32[4,512]{1,0:T(4,128)S(1)}, s32[4,512]{1,0:T(4,128)}, u32[]{:S(2)}) copy-start(s32[4,512]{1,0:T(4,128)} %param.16) | copy-start | bytes 24580
  64.1 53.9 %all-to-all-start.4 = ((bf16[16,128,896]{2,1,0:T(8,128)(2,1)}), bf16[16,128,896]{2,1,0:T(8,128)(2,1)}, u32[]{:S(2)}, u32[]{:S(2)}) async-start(bf16[16,128,896]{2,1,0:T(8,128)(2,1)} %broadcast_select_fusion), calls=%async_computation.4 | async-start | bytes 7340032 | tf_op jit(solution)/shard_map/all_to_all | solution.py:130
  67.4 813.4 %reduce-scatter.7.cloned.1.call-start = ((), (), s32[]{:S(2)}) async-start(), calls=%async_computation.13 | async-start | bytes 18522112 | tf_op jit(solution)/shard_map/reduce_scatter | solution.py:65
  145.2 10.5 %copy-start.35 = (f32[2048]{0:T(1024)}, f32[2048]{0:T(1024)S(1)}, u32[]{:S(2)}) copy-start(f32[2048]{0:T(1024)S(1)} %fusion.77) | copy-start | bytes 24580
  155.7 6.0 copy-start.4
  171.1 10.0 %copy-start.18 = (f32[512,32]{0,1:T(8,128)S(1)}, f32[512,32]{0,1:T(8,128)}, u32[]{:S(2)}) copy-start(f32[512,32]{0,1:T(8,128)} %get-tuple-element.203) | copy-start | bytes 196612
  171.1 10.0 %copy-start.20 = (f32[512,32]{0,1:T(8,128)S(1)}, f32[512,32]{0,1:T(8,128)}, u32[]{:S(2)}) copy-start(f32[512,32]{0,1:T(8,128)} %get-tuple-element.204) | copy-start | bytes 196612
  181.1 7.7 slice-start
  189.9 10.9 %copy-start.15 = (bf16[2048,128]{1,0:T(8,128)(2,1)S(1)}, bf16[2048,128]{1,0:T(8,128)(2,1)}, u32[]{:S(2)}) copy-start(bf16[2048,128]{1,0:T(8,128)(2,1)} %slice.130) | copy-start | bytes 1572868
  190.0 14.7 %copy-start.10 = (pred[512,512]{0,1:T(8,128)(4,1)S(1)}, pred[512,512]{0,1:T(8,128)(4,1)}, u32[]{:S(2)}) copy-start(pred[512,512]{0,1:T(8,128)(4,1)} %iota_compare_fusion.7) | copy-start | bytes 786436
  194.3 10.5 %copy-start.5 = (bf16[4,512,14,32]{1,3,2,0:T(8,128)(2,1)S(1)}, bf16[4,512,14,32]{1,3,2,0:T(8,128)(2,1)}, u32[]{:S(2)}) copy-start(bf16[4,512,14,32]{1,3,2,0:T(8,128)(2,1)} %copy.97) | copy-start | bytes 5505028
  203.3 72.9 %copy-start.13 = (bf16[4,512,2,64]{1,0,3,2:T(4,128)(2,1)}, bf16[4,512,2,64]{1,0,3,2:T(4,128)(2,1)S(1)}, u32[]{:S(2)}) copy-start(bf16[4,512,2,64]{1,0,3,2:T(4,128)(2,1)S(1)} %reshape.457) | copy-start | bytes 1572868
  204.7 22.4 %copy-start.24 = (bf16[4,512,2,32]{1,3,2,0:T(8,128)(2,1)}, bf16[4,512,2,32]{1,3,2,0:T(8,128)(2,1)S(1)}, u32[]{:S(2)}) copy-start(bf16[4,512,2,32]{1,3,2,0:T(8,128)(2,1)S(1)} %get-tuple-element.192) | copy-start | bytes 786436
  204.7 22.3 %copy-start.26 = (bf16[4,512,2,32]{1,3,2,0:T(8,128)(2,1)}, bf16[4,512,2,32]{1,3,2,0:T(8,128)(2,1)S(1)}, u32[]{:S(2)}) copy-start(bf16[4,512,2,32]{1,3,2,0:T(8,128)(2,1)S(1)} %get-tuple-element.193) | copy-start | bytes 786436
  227.0 19.2 %copy-start.22 = (f32[4,2,7,512]{3,2,1,0:T(8,128)}, f32[4,2,7,512]{3,2,1,0:T(8,128)S(1)}, u32[]{:S(2)}) copy-start(f32[4,2,7,512]{3,2,1,0:T(8,128)S(1)} %get-tuple-element.205) | copy-start | bytes 344068
  246.3 29.9 %copy-start.16 = (f32[4,2,7,512]{3,2,1,0:T(8,128)}, f32[4,2,7,512]{3,2,1,0:T(8,128)S(1)}, u32[]{:S(2)}) copy-start(f32[4,2,7,512]{3,2,1,0:T(8,128)S(1)} %fusion.24) | copy-start | bytes 344068
  523.6 359.1 %reduce-scatter.9.cloned.1.call-start = ((), (), s32[]{:S(2)}) async-start(), calls=%async_computation.14 | async-start | bytes 37044224 | tf_op jit(solution)/shard_map/reduce_scatter | solution.py:65
  524.5 53.0 %copy-start.38 = (f32[2048]{0:T(1024)S(1)}, f32[2048]{0:T(1024)}, u32[]{:S(2)}) copy-start(f32[2048]{0:T(1024)} %copy-done.37) | copy-start | bytes 24580
  524.5 53.0 %copy-start.8 = (bf16[4,512,896]{2,1,0:T(8,128)(2,1)S(1)}, bf16[4,512,896]{2,1,0:T(8,128)(2,1)}, u32[]{:S(2)}) copy-start(bf16[4,512,896]{2,1,0:T(8,128)(2,1)} %param.17) | copy-start | bytes 11010052
  577.5 6.5 copy-start.43
  582.1 1.9 copy-start.1
  589.9 13.4 %copy-start.11 = (pred[512,512]{0,1:T(8,128)(4,1)S(1)}, pred[512,512]{0,1:T(8,128)(4,1)}, u32[]{:S(2)}) copy-start(pred[512,512]{0,1:T(8,128)(4,1)} %iota_compare_fusion.7) | copy-start | bytes 786436
  589.9 13.4 %copy-start.14 = (bf16[4,512,2,64]{1,0,3,2:T(4,128)(2,1)S(1)}, bf16[4,512,2,64]{1,0,3,2:T(4,128)(2,1)}, u32[]{:S(2)}) copy-start(bf16[4,512,2,64]{1,0,3,2:T(4,128)(2,1)} %copy-done.13) | copy-start | bytes 1572868
  589.9 13.4 %copy-start.23 = (f32[4,2,7,512]{3,2,1,0:T(8,128)S(1)}, f32[4,2,7,512]{3,2,1,0:T(8,128)}, u32[]{:S(2)}) copy-start(f32[4,2,7,512]{3,2,1,0:T(8,128)} %copy-done.22) | copy-start | bytes 344068
  640.5 39.5 %copy-start.25 = (bf16[4,512,2,32]{1,3,2,0:T(8,128)(2,1)S(1)}, bf16[4,512,2,32]{1,3,2,0:T(8,128)(2,1)}, u32[]{:S(2)}) copy-start(bf16[4,512,2,32]{1,3,2,0:T(8,128)(2,1)} %copy-done.24) | copy-start | bytes 786436
  640.5 39.5 %copy-start.27 = (bf16[4,512,2,32]{1,3,2,0:T(8,128)(2,1)S(1)}, bf16[4,512,2,32]{1,3,2,0:T(8,128)(2,1)}, u32[]{:S(2)}) copy-start(bf16[4,512,2,32]{1,3,2,0:T(8,128)(2,1)} %copy-done.26) | copy-start | bytes 786436
  701.8 2.0 copy-start.7
  717.3 2.0 copy-start
  734.5 10.4 %copy-start.9 = (bf16[2048,1152]{0,1:T(8,128)(2,1)}, bf16[2048,1152]{0,1:T(8,128)(2,1)S(1)}, u32[]{:S(2)}) copy-start(bf16[2048,1152]{0,1:T(8,128)(2,1)S(1)} %constant_dynamic-update-slice_fusion) | copy-start | bytes 14155780
  734.5 10.5 %copy-start.32 = (f32[2048]{0:T(1024)S(1)}, f32[2048]{0:T(1024)}, u32[]{:S(2)}) copy-start(f32[2048]{0:T(1024)} %copy-done.31) | copy-start | bytes 24580
  734.5 10.5 %copy-start.2 = (bf16[2048,896]{1,0:T(8,128)(2,1)S(1)}, bf16[2048,896]{1,0:T(8,128)(2,1)}, u32[]{:S(2)}) copy-start(bf16[2048,896]{1,0:T(8,128)(2,1)} %copy-done.1) | copy-start | bytes 11010052
  745.0 4.3 copy-start.41
  749.3 11.5 %copy-start.3 = (bf16[2048,896]{1,0:T(8,128)(2,1)}, bf16[2048,896]{1,0:T(8,128)(2,1)S(1)}, u32[]{:S(2)}) copy-start(bf16[2048,896]{1,0:T(8,128)(2,1)S(1)} %fusion.45) | copy-start | bytes 11010052
  760.9 3.9 copy-start.42
  760.9 11.4 %slice-start.1 = ((s8[4718592]{0:T(1024)(128)(4,1)}), s8[524288]{0:T(1024)(128)(4,1)S(1)}, s32[]{:S(2)}) async-start(s8[4718592]{0:T(1024)(128)(4,1)} %bitcast.181), calls=%async_computation.17 | async-start | bytes 1048576
  760.9 119.8 %all-to-all-start.5 = ((f32[16,128,896]{2,1,0:T(8,128)}), f32[16,128,896]{2,1,0:T(8,128)}, u32[]{:S(2)}, u32[]{:S(2)}) async-start(f32[16,128,896]{2,1,0:T(8,128)} %bitcast.172), calls=%async_computation.7 | async-start | bytes 14680064 | tf_op jit(solution)/shard_map/all_to_all | solution.py:185
  764.7 204.5 %reduce-scatter.11.cloned.1.call-start = ((), (), s32[]{:S(2)}) async-start(), calls=%async_computation.15 | async-start | bytes 8286208
  765.0 7.3 slice-start.2
  884.4 86.6 %collective-permute-start.1 = (bf16[56,9728]{1,0:T(8,128)(2,1)S(1)}, bf16[56,9728]{1,0:T(8,128)(2,1)S(1)}, u32[]{:S(2)}, u32[]{:S(2)}) collective-permute-start(bf16[56,9728]{1,0:T(8,128)(2,1)S(1)} %convert_element_type.236), channel_id=1, source_target_pairs={{0,0},{1,1},{2,2},{3,3},{6,4},{7,5},{4,6},{5,7},{12,8},{13,9},{14,... | collective-permute-start | bytes 3268616 | tf_op jit(solution)/shard_map/ppermute | solution.py:69
  886.4 28.3 %copy-start.30 = (s32[16,1,128]{2,1,0:T(1,128)S(1)}, s32[16,1,128]{2,1,0:T(1,128)}, u32[]{:S(2)}) copy-start(s32[16,1,128]{2,1,0:T(1,128)} %copy-done.29) | copy-start | bytes 24580
  886.4 28.3 %copy-start.34 = (s32[4,512]{1,0:T(4,128)S(1)}, s32[4,512]{1,0:T(4,128)}, u32[]{:S(2)}) copy-start(s32[4,512]{1,0:T(4,128)} %param.16) | copy-start | bytes 24580
  886.5 78.1 %collective-permute-start.2 = (bf16[304,896]{1,0:T(8,128)(2,1)S(1)}, bf16[304,896]{1,0:T(8,128)(2,1)S(1)}, u32[]{:S(2)}, u32[]{:S(2)}) collective-permute-start(bf16[304,896]{1,0:T(8,128)(2,1)S(1)} %convert_element_type.237), channel_id=1, source_target_pairs={{0,0},{1,1},{2,2},{3,3},{6,4},{7,5},{4,6},{5,7},{12,8},{13,9},{14,... | collective-permute-start | bytes 1634312 | tf_op jit(solution)/shard_map/ppermute | solution.py:69
  970.3 1.7 collective-permute-start
  (11 other events, 13.2 us)
Sparse Core Ops, SparseCore 0:
  11.7 32.1 all-gather.6
  46.1 36.8 all-gather.8
  85.2 65.0 all-gather.12
  152.4 78.1 all-gather.10
  523.7 96.3 reduce-scatter.6
  622.3 260.2 reduce-scatter.8
  885.0 84.1 reduce-scatter.10
